TPU v7x, 32 devices: a whole 2x2x4 slice. The times are simulated.
32 devices in a mesh: groups: 2 (over x), seq: 16 (over z, y, core).
Axes of the slice: x: 2, y: 2, z: 4, core: 2. Of those that a mesh axis runs over, the one named last changes fastest.
Arguments:
- query: bfloat16 [16, 4096], P('groups'), parts along dimension 0, may hold values from -12 to 12
- new_key: bfloat16 [16, 1024], P('groups'), parts along dimension 0, may hold values from -12 to 12
- new_value: bfloat16 [16, 1024], P('groups'), parts along dimension 0, may hold values from -12 to 12
- cache_keys: bfloat16 [16, 1024, 1024], P('groups', 'seq'), parts along dimension 0, may hold values from -6 to 6
- cache_values: bfloat16 [16, 1024, 1024], P('groups', 'seq'), parts along dimension 0, may hold values from -6 to 6
- cache_lengths: int32 [16], P('groups'), parts along dimension 0, may hold values from 512 to 1024
- residual_input: bfloat16 [16, 4096], P('groups'), parts along dimension 0, may hold values from -6 to 6
- w_out: bfloat16 [4096, 4096], P('seq'), may hold values from -0.09375 to 0.09375
- norm_gain: bfloat16 [4096], replicated, may hold values from 0.099609375 to 1.8984375
- w_router: bfloat16 [4096, 4], replicated, may hold values from -0.09375 to 0.09375
- w_gate: bfloat16 [4096, 28672], P(None, 'seq'), may hold values from -0.09375 to 0.09375
- w_up: bfloat16 [4096, 28672], P(None, 'seq'), may hold values from -0.09375 to 0.09375
- expert_down_weight: bfloat16 [28672, 4096], P('seq'), may hold values from -0.09375 to 0.09375
- expert_ids: int32 [16, 2], P('groups'), parts along dimension 0, may hold values from 0 to 3, all different within a row
Outputs:
- attn_proj: bfloat16 [16, 4096], P('groups', 'seq'), parts along dimension 0
- layer_out: bfloat16 [16, 4096], P('groups', 'seq'), parts along dimension 0
There are 2 independent parts, one for each index of `groups`. A program takes and returns all parts, laid end to end along the dimension named above; an argument that names none is the same for every part. Nothing has to cross between parts.
Inputs may be any that keep to these rules, and one draw needn't show every extreme that they name: Cache positions 0 to cache_lengths[b] - 1 of sequence b are live, the rest are not read; the new key and value are always live. `expert_ids`: the two experts of a token differ.
All inputs are finite; a program needn't handle non-finite values.
Results may differ from a plain program's by a relative error of at most 0.012.
Values sent between devices are 32-bit elements; how exact they have to be, the bound alone decides.
A program may use at most 128 MiB of HBM per device.

v0:
```python
import math
import jax
import jax.numpy as jnp
from jax import lax
from jax.sharding import PartitionSpec as P

HEADS = 32
KV_HEADS = 8
HEAD_DIM = 128
FF = 7168
masked_score = -1e30


def joined(value, axis, join):
    pieces = jax.tree.map(lambda part: lax.all_gather(part, axis), value)
    head = jax.tree.map(lambda part: part[0], pieces)
    tail = jax.tree.map(lambda part: part[1:], pieces)
    so_far, _ = lax.scan(lambda so_far, share: (join(so_far, share), None), head, tail)
    return so_far


def merge_partial_results(first, second):
    first_max, first_sum, first_num = first
    second_max, second_sum, second_num = second
    ceiling = jnp.maximum(first_max, second_max)
    first_scale = jnp.exp(first_max - ceiling)
    second_scale = jnp.exp(second_max - ceiling)
    merged_sum = first_sum * first_scale + second_sum * second_scale
    merged_num = first_num * first_scale[..., None] + second_num * second_scale[..., None]
    return (ceiling, merged_sum, merged_num)


def per_device(
    query,
    new_key,
    new_value,
    cache_keys,
    cache_values,
    cache_lengths,
    residual_input,
    w_out,
    norm_gain,
    w_router,
    w_gate,
    w_up,
    expert_down_weight,
    expert_ids,
):
    seq_count = query.shape[0]
    per_group = HEADS // KV_HEADS
    local_len = cache_keys.shape[1]
    device = lax.axis_index("seq")
    inv_scale = 1.0 / math.sqrt(HEAD_DIM)
    query_vectors = query.reshape(seq_count, KV_HEADS, per_group, HEAD_DIM)
    key_block = cache_keys.reshape(seq_count, local_len, KV_HEADS, HEAD_DIM)
    value_block = cache_values.reshape(seq_count, local_len, KV_HEADS, HEAD_DIM)
    scores = (
        jnp.einsum("bkgd,btkd->bkgt", query_vectors, key_block, preferred_element_type=jnp.float32)
        * inv_scale
    )
    positions = device * local_len + jnp.arange(local_len, dtype=jnp.int32)
    is_live = (positions[None, :] < cache_lengths[:, None])[:, None, None, :]
    scores = jnp.where(is_live, scores, masked_score)
    incoming_key_rows = new_key.reshape(seq_count, KV_HEADS, HEAD_DIM)
    incoming_token_score = (
        jnp.einsum(
            "oqes,oqs->oqe", query_vectors, incoming_key_rows, preferred_element_type=jnp.float32
        )
        * inv_scale
    )
    fresh_value = new_value.astype(jnp.float32).reshape(seq_count, KV_HEADS, 1, HEAD_DIM)
    feat_width = w_out.shape[0]
    feat_start = device * feat_width
    flat_shape = (seq_count, HEADS * HEAD_DIM)
    local_max = jnp.max(scores, axis=-1)
    weights = jnp.where(is_live, jnp.exp(scores - local_max[..., None]), 0.0)
    numerator = jnp.einsum(
        "bkgt,btkd->bkgd",
        weights.astype(jnp.bfloat16),
        value_block,
        preferred_element_type=jnp.float32,
    )
    merged_max, merged_sum, merged_num = joined(
        (local_max, jnp.sum(weights, axis=-1), numerator), "seq", merge_partial_results
    )
    ceiling = jnp.maximum(merged_max, incoming_token_score)
    old_scale = jnp.exp(merged_max - ceiling)
    fresh_weight = jnp.exp(incoming_token_score - ceiling)
    fresh_rounded = lax.optimization_barrier(fresh_weight.astype(jnp.bfloat16)).astype(jnp.float32)
    numerator = merged_num * old_scale[..., None] + fresh_rounded[..., None] * fresh_value
    denominator = merged_sum * old_scale + fresh_weight
    context = (numerator / denominator[..., None]).reshape(flat_shape)
    context_own = lax.dynamic_slice_in_dim(context, feat_start, feat_width, 1).astype(jnp.bfloat16)
    projected = lax.psum(jnp.dot(context_own, w_out, preferred_element_type=jnp.float32), "seq")
    out_width = projected.shape[1] // lax.axis_size("seq")
    out_start = device * out_width
    attn_proj = lax.dynamic_slice_in_dim(projected, out_start, out_width, 1).astype(jnp.bfloat16)
    stream = residual_input.astype(jnp.float32) + projected
    normed = (
        stream
        * lax.rsqrt(jnp.mean(stream * stream, axis=-1, keepdims=True) + 1e-05)
        * norm_gain.astype(jnp.float32)
    )
    normed = normed.astype(jnp.bfloat16)
    logits = jnp.dot(normed, w_router, preferred_element_type=jnp.float32)
    expert_count = w_router.shape[1]
    picks = expert_ids[:, :, None] == jnp.arange(expert_count, dtype=jnp.int32)[None, None, :]
    chosen = jnp.sum(jnp.where(picks, logits[:, None, :], 0.0), axis=-1)
    first_gate = jax.nn.sigmoid(chosen[:, 0] - chosen[:, 1])
    gate_pair = jnp.stack([first_gate, 1.0 - first_gate], axis=1)
    own_expert = device * w_gate.shape[1] // FF
    route_weight = jnp.sum(jnp.where(expert_ids == own_expert, gate_pair, 0.0), axis=1)
    gate_part = jnp.dot(normed, w_gate, preferred_element_type=jnp.float32)
    up_projection_share = jnp.dot(normed, w_up, preferred_element_type=jnp.float32)
    hidden = (jax.nn.silu(gate_part) * up_projection_share).astype(jnp.bfloat16)
    term = lax.dot_general(
        expert_down_weight, hidden, (((0,), (1,)), ((), ())), preferred_element_type=jnp.float32
    )
    moe_rows = lax.psum_scatter(
        term * route_weight[None, :], "seq", scatter_dimension=0, tiled=True
    )
    stream_own = lax.dynamic_slice_in_dim(stream, out_start, out_width, 1)
    layer_out = (stream_own + moe_rows.T).astype(jnp.bfloat16)
    return (attn_proj, layer_out)


def solution(mesh):
    placed = (
        P("groups", None),
        P("groups", None),
        P("groups", None),
        P("groups", "seq", None),
        P("groups", "seq", None),
        P("groups"),
        P("groups", None),
        P("seq", None),
        P(),
        P(),
        P(None, "seq"),
        P(None, "seq"),
        P("seq", None),
        P("groups", None),
    )
    return jax.shard_map(
        per_device,
        mesh=mesh,
        in_specs=placed,
        out_specs=(P("groups", "seq"), P("groups", "seq")),
        check_vma=False,
    )
```

profile of v0, /device:TPU:0, one launch (start us, length us, event | category | flops | bytes accessed | tf_op | source)
XLA Modules:
  0.0 263.8 jit_solution(7450599788652511796)
XLA Ops:
  7.3 0.9 broadcast_compare_fusion
  8.1 2.0 fusion.38
  10.1 1.7 fusion.7
  11.8 0.7 copy.51
  12.7 0.3 fusion.13
  13.1 24.1 %all-gather.1 = f32[128,8,4]{1,2,0:T(4,128)S(1)} all-gather(f32[8,8,4]{1,2,0:T(4,128)S(1)} %copy.49), channel_id=3, replica_groups=mesh['groups'=2,'seq'=16] {'seq'}, dimensions={0}, use_global_device_ids=true | all-gather | bytes 17408 | tf_op jit(solution)/shard_map/all_gather | solution.py:15
  37.2 18.7 %all-gather = f32[128,8,4]{1,2,0:T(4,128)S(1)} all-gather(f32[8,8,4]{1,2,0:T(4,128)S(1)} %copy.48), channel_id=2, replica_groups=mesh['groups'=2,'seq'=16] {'seq'}, dimensions={0}, use_global_device_ids=true | all-gather | bytes 17408 | tf_op jit(solution)/shard_map/all_gather | solution.py:15
  56.0 1.0 fusion.23
  57.2 0.7 bitcast_convert_fusion
  57.9 0.9 slice.40
  58.9 3.0 %slice.43 = f32[120,8,4,128]{3,1,2,0:T(8,128)} slice(f32[128,8,4,128]{3,1,2,0:T(8,128)} %all-gather.5.cloned.1.call-done), slice={[8:128], [0:8], [0:4], [0:128]} | slice | bytes 3932160 | tf_op jit(solution)/shard_map/slice | solution.py:17
  61.9 24.5 %while.14 = (s32[]{:T(128)}, f32[8,8,4]{1,2,0:T(4,128)S(1)}, f32[8,8,4]{1,2,0:T(4,128)S(1)}, f32[8,8,4,128]{3,2,1,0:T(4,128)S(1)}, f32[15,8,8,4]{2,3,1,0:T(4,128...) while((s32[]{:T(128)}, f32[8,8,4]{1,2,0:T(4,128)S(1)}, ...), condition=%wide.region_3.4_spmd, body=%wide.region_2.3_spmd.sunk | while | flops 99842 | bytes 669797 | solution.py:18
  62.1 0.9 constant_dynamic-slice_fusion.2
  63.0 0.4 fusion.54
  63.5 0.1 copy.90
  63.8 0.9 constant_dynamic-slice_fusion.2
  64.7 0.4 fusion.54
  65.2 0.1 copy.90
  65.3 0.1 copy.91
  65.4 0.9 constant_dynamic-slice_fusion.2
  66.3 0.4 fusion.54
  67.0 0.9 constant_dynamic-slice_fusion.2
  68.0 0.4 fusion.54
  68.4 0.1 copy.90
  68.6 0.1 copy.91
  68.7 0.9 constant_dynamic-slice_fusion.2
  69.6 0.4 fusion.54
  70.3 0.9 constant_dynamic-slice_fusion.2
  71.2 0.4 fusion.54
  71.7 0.1 copy.90
  71.8 0.1 copy.91
  72.0 0.9 constant_dynamic-slice_fusion.2
  72.9 0.4 fusion.54
  73.4 0.1 copy.90
  73.5 0.1 copy.91
  73.6 0.9 constant_dynamic-slice_fusion.2
  74.5 0.4 fusion.54
  75.2 0.9 constant_dynamic-slice_fusion.2
  76.1 0.4 fusion.54
  76.6 0.1 copy.90
  76.9 0.9 constant_dynamic-slice_fusion.2
  77.8 0.4 fusion.54
  78.5 0.9 constant_dynamic-slice_fusion.2
  79.4 0.4 fusion.54
  80.1 0.9 constant_dynamic-slice_fusion.2
  81.1 0.4 fusion.54
  81.8 0.9 constant_dynamic-slice_fusion.2
  82.7 0.4 fusion.54
  83.4 0.9 constant_dynamic-slice_fusion.2
  84.3 0.4 fusion.54
  85.1 0.9 constant_dynamic-slice_fusion.2
  86.0 0.4 fusion.54
  86.4 0.1 copy.54
  86.7 0.1 copy.55
  86.8 0.3 add_divide_fusion
  87.1 1.0 fusion.31
  88.3 87.4 %all-reduce.2.cloned.1.call-done = f32[8,4096]{1,0:T(8,128)} async-done(((f32[8,4096]{1,0:T(8,128)}), f32[8,4096]{1,0:T(8,128)}) %all-reduce.2.cloned.1.call-update) | async-done | bytes 131088 | tf_op jit(solution)/shard_map/psum | solution.py:94
  175.8 1.1 multiply_reduce_fusion
  176.9 0.1 fusion.40
  177.1 7.2 %fusion.39 = f32[8,1792]{1,0:T(8,128)S(1)} fusion(bf16[8,4096]{1,0:T(8,128)(2,1)S(1)} %multiply_convert_fusion, bf16[4096,1792]{1,0:T(8,128)(2,1)} %param.26), kind=kOutput, calls=%fused_computation.67 | convolution fusion | flops 117440512 | bytes 14802944 | tf_op jit(solution)/shard_map/dot_general | solution.py:113
  184.3 14.3 %fusion.4 = f32[4096,8]{0,1:T(8,128)} fusion(bf16[1792,4096]{1,0:T(8,128)(2,1)} %param.28, bf16[8,4096]{1,0:T(8,128)(2,1)S(1)} %multiply_convert_fusion, bf16[4096,1792]{1,0:T(8,128)(2,1)} %param.27, f32[8]{0:T(128)S(1)} %fusion.32, f32[8,1792]{1,0:T(8,128)S(1)} %fusion.39), kind=kOutput, calls=%fused_computation.11 | convolution fusion | flops 234999808 | bytes 29614112 | tf_op jit(solution)/shard_map/dot_general | solution.py:116
  198.6 1.3 dynamic-slice_convert_fusion
  199.9 56.0 %reduce-scatter.2.cloned.1.call-done = f32[256,8]{0,1:T(8,128)} async-done(((f32[4096,8]{0,1:T(8,128)}), f32[256,8]{0,1:T(8,128)}) %reduce-scatter.2.cloned.1.call-update) | async-done | bytes 8208 | tf_op jit(solution)/shard_map/reduce_scatter | solution.py:119
  255.9 1.3 fusion.30
  (71 shorter events, 4.0 us)
Async XLA Ops:
  7.2 80.0 %copy-start = (bf16[256,4096]{1,0:T(8,128)(2,1)S(1)}, bf16[256,4096]{1,0:T(8,128)(2,1)}, u32[]{:S(2)}) copy-start(bf16[256,4096]{1,0:T(8,128)(2,1)} %param.23) | copy-start | bytes 6291460
  7.2 81.1 %copy-start.2 = (bf16[4096]{0:T(1024)(128)(2,1)S(1)}, bf16[4096]{0:T(1024)(128)(2,1)}, u32[]{:S(2)}) copy-start(bf16[4096]{0:T(1024)(128)(2,1)} %param.24) | copy-start | bytes 24580
  7.2 168.6 %copy-start.1 = (bf16[8,4096]{1,0:T(8,128)(2,1)S(1)}, bf16[8,4096]{1,0:T(8,128)(2,1)}, u32[]{:S(2)}) copy-start(bf16[8,4096]{1,0:T(8,128)(2,1)} %param.22) | copy-start | bytes 196612
  7.2 169.7 %copy-start.4 = (bf16[4096,4]{0,1:T(4,128)(2,1)S(1)}, bf16[4096,4]{0,1:T(4,128)(2,1)}, u32[]{:S(2)}) copy-start(bf16[4096,4]{0,1:T(4,128)(2,1)} %param.25) | copy-start | bytes 98308
  7.2 169.9 %copy-start.3 = (s32[8,2]{0,1:T(2,128)S(1)}, s32[8,2]{0,1:T(2,128)}, u32[]{:S(2)}) copy-start(s32[8,2]{0,1:T(2,128)} %param.29) | copy-start | bytes 196
  7.2 50.7 %all-gather.5.cloned.1.call-start = ((), (), s32[]{:S(2)}) async-start(), calls=%async_computation.3 | async-start | bytes 2228224 | tf_op jit(solution)/shard_map/all_gather | solution.py:15
  12.5 163.2 %all-reduce.2.cloned.1.call-start = ((), (), s32[]{:S(2)}) async-start(), calls=%async_computation.1 | async-start | bytes 262144 | tf_op jit(solution)/shard_map/psum | solution.py:94
  88.2 167.7 %reduce-scatter.2.cloned.1.call-start = ((), (), s32[]{:S(2)}) async-start(), calls=%async_computation.2 | async-start | bytes 139264 | tf_op jit(solution)/shard_map/reduce_scatter | solution.py:119
Sparse Core Ops, SparseCore 0:
  12.6 44.5 all-gather.4
  88.3 87.3 all-reduce.1
  198.7 57.1 reduce-scatter.1
where the time goes:
time: 265 us; the launch traced here: 264 us
  waiting for transfers between devices  144 us (54%)
  blocking collectives  42.9 us (16%)
  matrix products  27.3 us (10%)
  local copies, waits for them, and re-layouts  24.1 us (9%)
  between operations  14 us (5%)
  other arithmetic  11.7 us (4%)
    psum x1, waiting for transfers between devices, per_device(): lax.psum(jnp.dot(context_own, w_out, preferred_element_type=jnp.float32),...  87.4 us
    reduce_scatter x1, waiting for transfers between devices, per_device(): lax.psum_scatter(term * route_weight[None, :], 'seq', scatter_dimension=0...  56 us
    all_gather x2, blocking collectives, joined(): pieces = jax.tree.map(lambda part: lax.all_gather(part, axis), value)  42.9 us
    dot_general x1, matrix products, per_device(): lax.dot_general(expert_down_weight, hidden, (((0,), (1,)), ((), ())), pre...  14.3 us
    dynamic_slice x15, local copies, waits for them, and re-layouts, joined(): lax.scan(lambda so_far, share: (join(so_far, share), None), head, tail)  13.7 us
    dot_general x1, matrix products, per_device(): gate_part = jnp.dot(normed, w_gate, preferred_element_type=jnp.float32)  7.18 us
    add x15, other arithmetic, merge_partial_results(): first_num * first_scale[..., None] + second_num * second_scale[..., None]  6.37 us
  transfers between devices with their start and end apart: 3, of which 2 were waited for; matrix products, arithmetic and copies ran while one was open for 1% of the time, Pallas kernels for 0%

commit v1 on v0

--- a/solution.py
+++ b/solution.py
@@ -91,7 +91,10 @@
     denominator = merged_sum * old_scale + fresh_weight
     context = (numerator / denominator[..., None]).reshape(flat_shape)
     context_own = lax.dynamic_slice_in_dim(context, feat_start, feat_width, 1).astype(jnp.bfloat16)
-    projected = lax.psum(jnp.dot(context_own, w_out, preferred_element_type=jnp.float32), "seq")
+    projected = jnp.sum(
+        lax.all_gather(jnp.dot(context_own, w_out, preferred_element_type=jnp.float32), "seq"),
+        axis=0,
+    )
     out_width = projected.shape[1] // lax.axis_size("seq")
     out_start = device * out_width
     attn_proj = lax.dynamic_slice_in_dim(projected, out_start, out_width, 1).astype(jnp.bfloat16)

time: 265 us -> 216 us (0.82)
  waiting for transfers between devices: 144 us -> 94.6 us
    psum x1 -> x0, waiting for transfers between devices: 87.4 us -> none  [per_device(): lax.psum(jnp.dot(context_own, w_out, preferred_element_type=jnp.float32),...]
    all_gather x0 -> x1, waiting for transfers between devices: none -> 40.6 us  [per_device(): lax.all_gather(jnp.dot(context_own, w_out, preferred_element_type=jnp.flo...]
where the time goes in v1:
time: 216 us; the launch traced here: 215 us
  waiting for transfers between devices  94.6 us (44%)
  blocking collectives  42.9 us (20%)
  matrix products  27.3 us (13%)
  local copies, waits for them, and re-layouts  23.4 us (11%)
  between operations  14 us (6%)
  other arithmetic  12.5 us (6%)
    reduce_scatter x1, waiting for transfers between devices, per_device(): lax.psum_scatter(term * route_weight[None, :], 'seq', scatter_dimension=0...  53.9 us
    all_gather x2, blocking collectives, joined(): pieces = jax.tree.map(lambda part: lax.all_gather(part, axis), value)  42.9 us
    all_gather x1, waiting for transfers between devices, per_device(): lax.all_gather(jnp.dot(context_own, w_out, preferred_element_type=jnp.flo...  40.6 us
    dot_general x1, matrix products, per_device(): lax.dot_general(expert_down_weight, hidden, (((0,), (1,)), ((), ())), pre...  14.2 us
    dynamic_slice x15, local copies, waits for them, and re-layouts, joined(): lax.scan(lambda so_far, share: (join(so_far, share), None), head, tail)  13.7 us
    dot_general x1, matrix products, per_device(): gate_part = jnp.dot(normed, w_gate, preferred_element_type=jnp.float32)  7.18 us
    add x15, other arithmetic, merge_partial_results(): first_num * first_scale[..., None] + second_num * second_scale[..., None]  6.37 us
  transfers between devices with their start and end apart: 3, of which 2 were waited for; matrix products, arithmetic and copies ran while one was open for 1% of the time, Pallas kernels for 0%

profile of v1, /device:TPU:0, one launch (start us, length us, event | category | flops | bytes accessed | tf_op | source)
XLA Modules:
  0.0 214.9 jit_solution(10120236217589581840)
XLA Ops:
  7.3 0.9 broadcast_compare_fusion
  8.1 2.0 fusion.38
  10.1 1.7 fusion.7
  11.8 0.7 copy.51
  12.7 0.3 fusion.13
  13.1 24.1 %all-gather.1 = f32[128,8,4]{1,2,0:T(4,128)S(1)} all-gather(f32[8,8,4]{1,2,0:T(4,128)S(1)} %copy.49), channel_id=3, replica_groups=mesh['groups'=2,'seq'=16] {'seq'}, dimensions={0}, use_global_device_ids=true | all-gather | bytes 17408 | tf_op jit(solution)/shard_map/all_gather | solution.py:15
  37.2 18.7 %all-gather = f32[128,8,4]{1,2,0:T(4,128)S(1)} all-gather(f32[8,8,4]{1,2,0:T(4,128)S(1)} %copy.48), channel_id=2, replica_groups=mesh['groups'=2,'seq'=16] {'seq'}, dimensions={0}, use_global_device_ids=true | all-gather | bytes 17408 | tf_op jit(solution)/shard_map/all_gather | solution.py:15
  56.0 1.0 fusion.23
  57.2 0.7 bitcast_convert_fusion
  57.9 0.9 slice.40
  58.9 3.0 %slice.43 = f32[120,8,4,128]{3,1,2,0:T(8,128)} slice(f32[128,8,4,128]{3,1,2,0:T(8,128)} %all-gather.7.cloned.1.call-done), slice={[8:128], [0:8], [0:4], [0:128]} | slice | bytes 3932160 | tf_op jit(solution)/shard_map/slice | solution.py:17
  61.9 24.5 %while.14 = (s32[]{:T(128)}, f32[8,8,4]{1,2,0:T(4,128)S(1)}, f32[8,8,4]{1,2,0:T(4,128)S(1)}, f32[8,8,4,128]{3,2,1,0:T(4,128)S(1)}, f32[15,8,8,4]{2,3,1,0:T(4,128...) while((s32[]{:T(128)}, f32[8,8,4]{1,2,0:T(4,128)S(1)}, ...), condition=%wide.region_3.4_spmd, body=%wide.region_2.3_spmd.sunk | while | flops 99842 | bytes 669797 | solution.py:18
  62.1 0.9 constant_dynamic-slice_fusion.2
  63.0 0.4 fusion.54
  63.5 0.1 copy.90
  63.8 0.9 constant_dynamic-slice_fusion.2
  64.7 0.4 fusion.54
  65.2 0.1 copy.90
  65.3 0.1 copy.91
  65.4 0.9 constant_dynamic-slice_fusion.2
  66.3 0.4 fusion.54
  67.0 0.9 constant_dynamic-slice_fusion.2
  68.0 0.4 fusion.54
  68.4 0.1 copy.90
  68.6 0.1 copy.91
  68.7 0.9 constant_dynamic-slice_fusion.2
  69.6 0.4 fusion.54
  70.3 0.9 constant_dynamic-slice_fusion.2
  71.2 0.4 fusion.54
  71.7 0.1 copy.90
  71.8 0.1 copy.91
  72.0 0.9 constant_dynamic-slice_fusion.2
  72.9 0.4 fusion.54
  73.4 0.1 copy.90
  73.5 0.1 copy.91
  73.6 0.9 constant_dynamic-slice_fusion.2
  74.5 0.4 fusion.54
  75.2 0.9 constant_dynamic-slice_fusion.2
  76.1 0.4 fusion.54
  76.9 0.9 constant_dynamic-slice_fusion.2
  77.8 0.4 fusion.54
  78.5 0.9 constant_dynamic-slice_fusion.2
  79.4 0.4 fusion.54
  80.1 0.9 constant_dynamic-slice_fusion.2
  81.1 0.4 fusion.54
  81.8 0.9 constant_dynamic-slice_fusion.2
  82.7 0.4 fusion.54
  83.4 0.9 constant_dynamic-slice_fusion.2
  84.3 0.4 fusion.54
  85.1 0.9 constant_dynamic-slice_fusion.2
  86.0 0.4 fusion.54
  86.4 0.1 copy.54
  86.7 0.1 copy.55
  86.8 0.3 add_divide_fusion
  87.1 1.0 fusion.31
  88.3 40.6 %all-gather.9.cloned.1.call-done = f32[128,4096]{1,0:T(8,128)} async-done(((f32[8,4096]{1,0:T(8,128)}), f32[128,4096]{1,0:T(8,128)}) %all-gather.9.cloned.1.call-update) | async-done | bytes 2097168 | tf_op jit(solution)/shard_map/all_gather | solution.py:95
  128.9 1.7 bitcast_reduce_fusion
  130.6 0.1 multiply_reduce_fusion
  130.8 0.1 fusion.40
  131.0 7.2 %fusion.39 = f32[8,1792]{1,0:T(8,128)S(1)} fusion(bf16[8,4096]{1,0:T(8,128)(2,1)S(1)} %multiply_convert_fusion, bf16[4096,1792]{1,0:T(8,128)(2,1)} %param.26), kind=kOutput, calls=%fused_computation.68 | convolution fusion | flops 117440512 | bytes 14802944 | tf_op jit(solution)/shard_map/dot_general | solution.py:116
  138.2 14.2 %fusion.4 = f32[4096,8]{0,1:T(8,128)} fusion(bf16[1792,4096]{1,0:T(8,128)(2,1)} %param.28, bf16[8,4096]{1,0:T(8,128)(2,1)S(1)} %multiply_convert_fusion, bf16[4096,1792]{1,0:T(8,128)(2,1)} %param.27, f32[8]{0:T(128)S(1)} %fusion.32, f32[8,1792]{1,0:T(8,128)S(1)} %fusion.39), kind=kOutput, calls=%fused_computation.11 | convolution fusion | flops 234999808 | bytes 29614112 | tf_op jit(solution)/shard_map/dot_general | solution.py:119
  152.5 0.6 dynamic-slice_convert_fusion
  153.1 53.9 %reduce-scatter.2.cloned.1.call-done = f32[256,8]{0,1:T(8,128)} async-done(((f32[4096,8]{0,1:T(8,128)}), f32[256,8]{0,1:T(8,128)}) %reduce-scatter.2.cloned.1.call-update) | async-done | bytes 8208 | tf_op jit(solution)/shard_map/reduce_scatter | solution.py:122
  207.1 1.3 fusion.30
  (72 shorter events, 4.2 us)
Async XLA Ops:
  7.2 80.0 %copy-start = (bf16[256,4096]{1,0:T(8,128)(2,1)S(1)}, bf16[256,4096]{1,0:T(8,128)(2,1)}, u32[]{:S(2)}) copy-start(bf16[256,4096]{1,0:T(8,128)(2,1)} %param.23) | copy-start | bytes 6291460
  7.2 81.1 %copy-start.2 = (bf16[4096]{0:T(1024)(128)(2,1)S(1)}, bf16[4096]{0:T(1024)(128)(2,1)}, u32[]{:S(2)}) copy-start(bf16[4096]{0:T(1024)(128)(2,1)} %param.24) | copy-start | bytes 24580
  7.2 123.4 %copy-start.1 = (bf16[8,4096]{1,0:T(8,128)(2,1)S(1)}, bf16[8,4096]{1,0:T(8,128)(2,1)}, u32[]{:S(2)}) copy-start(bf16[8,4096]{1,0:T(8,128)(2,1)} %param.22) | copy-start | bytes 196612
  7.2 123.6 %copy-start.4 = (bf16[4096,4]{0,1:T(4,128)(2,1)S(1)}, bf16[4096,4]{0,1:T(4,128)(2,1)}, u32[]{:S(2)}) copy-start(bf16[4096,4]{0,1:T(4,128)(2,1)} %param.25) | copy-start | bytes 98308
  7.2 123.8 %copy-start.3 = (s32[8,2]{0,1:T(2,128)S(1)}, s32[8,2]{0,1:T(2,128)}, u32[]{:S(2)}) copy-start(s32[8,2]{0,1:T(2,128)} %param.29) | copy-start | bytes 196
  7.2 50.7 %all-gather.7.cloned.1.call-start = ((), (), s32[]{:S(2)}) async-start(), calls=%async_computation.2 | async-start | bytes 2228224 | tf_op jit(solution)/shard_map/all_gather | solution.py:15
  12.5 116.4 %all-gather.9.cloned.1.call-start = ((), (), s32[]{:S(2)}) async-start(), calls=%async_computation.3 | async-start | bytes 2228224 | tf_op jit(solution)/shard_map/all_gather | solution.py:95
  88.2 118.9 %reduce-scatter.2.cloned.1.call-start = ((), (), s32[]{:S(2)}) async-start(), calls=%async_computation.1 | async-start | bytes 139264 | tf_op jit(solution)/shard_map/reduce_scatter | solution.py:122
Sparse Core Ops, SparseCore 0:
  12.6 44.5 all-gather.6
  88.3 40.4 all-gather.8
  152.6 54.3 reduce-scatter.1
